TPU v7x, 32 devices: a whole 2x2x4 slice. The times are simulated.
32 devices in a mesh: row: 4 (over z), col: 8 (over y, x, core).
Axes of the slice: x: 2, y: 2, z: 4, core: 2. Of those that a mesh axis runs over, the one named last changes fastest.
Arguments:
- grad_terms: bfloat16 [8, 2, 4096, 10240], P('col', None, 'row'), may hold values from -25 to 25, as said below
- row_moment: float32 [2, 4096], P(None, 'row'), may hold values from 0.01 to 3
- col_moment: float32 [2, 10240], P(None, 'col'), may hold values from 0.01 to 1
Outputs:
- update: float32 [2, 4096, 10240], P(None, 'row', 'col')
- new_rows: float32 [2, 4096], P(None, 'row')
- new_cols: float32 [2, 10240], P(None, 'col')
Inputs may be any that keep to these rules, and one draw needn't show every extreme that they name: `grad_terms`: partial gradient terms of the 8 batch shards.
All inputs are finite; a program needn't handle non-finite values.
Results may differ from a plain program's by a relative error of at most 0.0003.
Values sent between devices are 32-bit elements; how exact they have to be, the bound alone decides.
No kernel may reach another device: no remote copies, remote signals or barrier semaphores. Data moves between devices by JAX's collectives and lax.ppermute only.
A program may use at most 256 MiB of HBM per device.

v0:
```python
import jax
import jax.numpy as jnp
from jax import lax
from jax.sharding import PartitionSpec as P

D = 4096
FF = 10240
second_decay = 1.0 - 100.0 ** (-0.8)
tiny_square = 1e-30


def on_device(grad_terms, row_moment, col_moment):
    partial_terms = grad_terms[0]
    gradient = lax.psum_scatter(
        partial_terms.astype(jnp.float32), "col", scatter_dimension=2, tiled=True
    )
    squares = gradient * gradient + tiny_square
    row_part = jnp.sum(squares, axis=2)
    col_part = jnp.sum(squares, axis=1)
    row_full = lax.psum(row_part, "col")
    col_full = lax.psum(col_part, "row")
    new_rows = second_decay * row_moment + (1.0 - second_decay) * row_full / FF
    new_cols = second_decay * col_moment + (1.0 - second_decay) * col_full / D
    row_level = lax.psum(jnp.sum(new_rows, axis=1), "row") / D
    estimate = new_rows[:, :, None] * new_cols[:, None, :] / row_level[:, None, None]
    raw_update = gradient / jnp.sqrt(estimate)
    clip_total = lax.psum(jnp.sum(raw_update * raw_update, axis=(1, 2)), ("row", "col"))
    clip_scale = jnp.maximum(1.0, jnp.sqrt(clip_total / (D * FF)))
    update = raw_update / clip_scale[:, None, None]
    return (update, new_rows, new_cols)


def solution(mesh):
    placed = (P("col", None, "row", None), P(None, "row"), P(None, "col"))
    return jax.shard_map(
        on_device,
        mesh=mesh,
        in_specs=placed,
        out_specs=(P(None, "row", "col"), P(None, "row"), P(None, "col")),
        check_vma=False,
    )
```

profile of v0, /device:TPU:10, one launch (start us, length us, event | category | flops | bytes accessed | tf_op | source)
XLA Modules:
  0.0 610.9 jit_solution(3607653950137789142)
XLA Ops:
  7.2 0.0 reduce-scatter.2.cloned.1.call-start
  7.2 40.9 %bitcast_convert_fusion = f32[2,1024,10240]{2,1,0:T(8,128)} fusion(bf16[1,2,1024,10240]{3,2,1,0:T(8,128)(2,1)} %param.3), kind=kLoop, calls=%fused_computation | loop fusion | flops 20971520 | bytes 125829120 | tf_op jit(solution)/shard_map/convert_element_type | solution.py:15
  48.1 0.0 reduce-scatter.2.cloned.1.call-update
  48.1 0.0 copy-start.3
  48.1 0.0 copy-start.2
  48.1 464.0 %reduce-scatter.2.cloned.1.call-done = f32[2,1024,1280]{2,1,0:T(8,128)} async-done(((f32[2,1024,10240]{2,1,0:T(8,128)}), f32[2,1024,1280]{2,1,0:T(8,128)}) %reduce-scatter.2.cloned.1.call-update) | async-done | bytes 10485776 | tf_op jit(solution)/shard_map/reduce_scatter | solution.py:14
  512.1 5.8 fusion
  517.9 10.3 %psum.28 = f32[2,1024]{1,0:T(2,128)S(1)} all-reduce(f32[2,1024]{1,0:T(2,128)S(1)} %get-tuple-element.4), channel_id=1, replica_groups=mesh['row'=4,'col'=8] {'col'}, use_global_device_ids=true, to_apply=%region_2.0 | all-reduce | flops 2048 | bytes 16384 | tf_op jit(solution)/shard_map/psum | solution.py:20
  528.1 0.0 copy-done.3
  528.1 0.1 fusion.2
  528.3 0.0 copy-start.1
  528.3 15.1 %all-reduce = (f32[2]{0:T(128)S(1)}, f32[2,1280]{1,0:T(2,128)S(1)}) all-reduce(f32[2]{0:T(128)S(1)} %get-tuple-element.7, f32[2,1280]{1,0:T(2,128)S(1)} %get-tuple-element.3), channel_id=1, replica_groups=mesh['row'=4,'col'=8] {'row'}, use_global_device_ids=true, to_apply=%region_6.0 | all-reduce | flops 2562 | bytes 20496 | tf_op jit(solution)/shard_map/psum | solution.py:24
  543.4 0.0 copy-done.2
  543.4 0.0 copy-start
  543.4 5.9 multiply_reduce_fusion
  549.4 45.0 %psum.31 = f32[2]{0:T(128)S(1)} all-reduce(f32[2]{0:T(128)S(1)} %multiply_reduce_fusion), channel_id=1, replica_groups=mesh['row'=4,'col'=8] {'row','col'}, use_global_device_ids=true, to_apply=%region_8.0 | all-reduce | flops 2 | bytes 16 | tf_op jit(solution)/shard_map/psum | solution.py:27
  594.4 9.6 %broadcast_divide_fusion = f32[2,1024,1280]{2,1,0:T(8,128)} fusion(f32[2]{0:T(128)S(1)} %sqrt_maximum_fusion, f32[2,1024,1280]{2,1,0:T(8,128)} %reduce-scatter.2.cloned.1.call-done, f32[2]{0:T(128)S(1)} %broadcast_multiply_fusion, f32[2,1280]{1,0:T(2,128)S(1)} %multiply_add_fusion.1, f32[2,1024]{1,0:T(2,128)S(1)} %get-tuple-element.8), kind=kLoop, calls=%fused_computation.6 | loop fusion | flops 10485760 | bytes 20989968 | tf_op jit(solution)/shard_map/div | solution.py:29
  604.0 0.0 copy-done.1
  604.0 0.0 copy-done
  (3 shorter events, 0.0 us)
Async XLA Ops:
  7.2 504.9 %reduce-scatter.2.cloned.1.call-start = ((), (), s32[]{:S(2)}) async-start(), calls=%async_computation.1 | async-start | bytes 94371840 | tf_op jit(solution)/shard_map/reduce_scatter | solution.py:14
  48.1 480.0 %copy-start.3 = (f32[2,1024]{1,0:T(2,128)S(1)}, f32[2,1024]{1,0:T(2,128)}, u32[]{:S(2)}) copy-start(f32[2,1024]{1,0:T(2,128)} %param.4) | copy-start | bytes 24580
  48.1 495.3 %copy-start.2 = (f32[2,1280]{1,0:T(2,128)S(1)}, f32[2,1280]{1,0:T(2,128)}, u32[]{:S(2)}) copy-start(f32[2,1280]{1,0:T(2,128)} %param.5) | copy-start | bytes 30724
  528.3 75.7 %copy-start.1 = (f32[2,1024]{1,0:T(2,128)}, f32[2,1024]{1,0:T(2,128)S(1)}, u32[]{:S(2)}) copy-start(f32[2,1024]{1,0:T(2,128)S(1)} %get-tuple-element.8) | copy-start | bytes 24580
  543.4 60.6 %copy-start = (f32[2,1280]{1,0:T(2,128)}, f32[2,1280]{1,0:T(2,128)S(1)}, u32[]{:S(2)}) copy-start(f32[2,1280]{1,0:T(2,128)S(1)} %multiply_add_fusion.1) | copy-start | bytes 30724
Sparse Core Ops, SparseCore 0:
  48.2 463.8 reduce-scatter.1
where the time goes:
time: 611 us
  waiting for transfers between devices  464 us (76%)
  blocking collectives  70.4 us (12%)
  other arithmetic  62.3 us (10%)
  between operations  14.1 us (2%)
    reduce_scatter x1, waiting for transfers between devices, on_device(): lax.psum_scatter(partial_terms.astype(jnp.float32), 'col', scatter_dimens...  464 us
    psum x1, blocking collectives, on_device(): lax.psum(jnp.sum(raw_update * raw_update, axis=(1, 2)), ('row', 'col'))  45 us
    convert_element_type x1, other arithmetic, on_device(): partial_terms.astype(jnp.float32)  40.9 us
    psum x1, blocking collectives, on_device(): row_level = lax.psum(jnp.sum(new_rows, axis=1), 'row') / D  15.1 us
  transfers between devices with their start and end apart: 1, of which 1 were waited for; matrix products, arithmetic and copies ran while one was open for 0% of the time, Pallas kernels for 0%

commit v1 on v0

--- a/solution.py
+++ b/solution.py
@@ -24,7 +24,13 @@
     row_level = lax.psum(jnp.sum(new_rows, axis=1), "row") / D
     estimate = new_rows[:, :, None] * new_cols[:, None, :] / row_level[:, None, None]
     raw_update = gradient / jnp.sqrt(estimate)
-    clip_total = lax.psum(jnp.sum(raw_update * raw_update, axis=(1, 2)), ("row", "col"))
+
+    def compute_fields(patch, mesh_ax, shard_axis):
+        for at in (mesh_ax, shard_axis):
+            patch = lax.psum(patch, at)
+        return patch
+
+    clip_total = compute_fields(jnp.sum(raw_update * raw_update, axis=(1, 2)), "row", "col")
     clip_scale = jnp.maximum(1.0, jnp.sqrt(clip_total / (D * FF)))
     update = raw_update / clip_scale[:, None, None]
     return (update, new_rows, new_cols)

time: 611 us -> 594 us (0.972)
  blocking collectives: 70.4 us -> 49.9 us
    psum x1 -> x2, blocking collectives: 45 us -> 24.5 us  [compute_fields(): patch = lax.psum(patch, at)]
where the time goes in v1:
time: 594 us; the launch traced here: 590 us
  waiting for transfers between devices  464 us (78%)
  other arithmetic  62.3 us (10%)
  blocking collectives  49.9 us (8%)
  between operations  14.1 us (2%)
    reduce_scatter x1, waiting for transfers between devices, on_device(): lax.psum_scatter(partial_terms.astype(jnp.float32), 'col', scatter_dimens...  464 us
    convert_element_type x1, other arithmetic, on_device(): partial_terms.astype(jnp.float32)  40.9 us
    psum x2, blocking collectives, compute_fields(): patch = lax.psum(patch, at)  24.5 us
    psum x1, blocking collectives, on_device(): row_level = lax.psum(jnp.sum(new_rows, axis=1), 'row') / D  15.1 us
  transfers between devices with their start and end apart: 1, of which 1 were waited for; matrix products, arithmetic and copies ran while one was open for 0% of the time, Pallas kernels for 0%

profile of v1, /device:TPU:10, one launch (start us, length us, event | category | flops | bytes accessed | tf_op | source)
XLA Modules:
  0.0 590.3 jit_solution(5969502915394997094)
XLA Ops:
  7.2 0.0 reduce-scatter.2.cloned.1.call-start
  7.2 40.9 %bitcast_convert_fusion = f32[2,1024,10240]{2,1,0:T(8,128)} fusion(bf16[1,2,1024,10240]{3,2,1,0:T(8,128)(2,1)} %param.3), kind=kLoop, calls=%fused_computation | loop fusion | flops 20971520 | bytes 125829120 | tf_op jit(solution)/shard_map/convert_element_type | solution.py:15
  48.1 0.0 reduce-scatter.2.cloned.1.call-update
  48.1 0.0 copy-start.3
  48.1 0.0 copy-start.2
  48.1 464.0 %reduce-scatter.2.cloned.1.call-done = f32[2,1024,1280]{2,1,0:T(8,128)} async-done(((f32[2,1024,10240]{2,1,0:T(8,128)}), f32[2,1024,1280]{2,1,0:T(8,128)}) %reduce-scatter.2.cloned.1.call-update) | async-done | bytes 10485776 | tf_op jit(solution)/shard_map/reduce_scatter | solution.py:14
  512.1 5.8 fusion
  517.9 10.3 %psum.35 = f32[2,1024]{1,0:T(2,128)S(1)} all-reduce(f32[2,1024]{1,0:T(2,128)S(1)} %get-tuple-element.4), channel_id=1, replica_groups=mesh['row'=4,'col'=8] {'col'}, use_global_device_ids=true, to_apply=%region_2.0 | all-reduce | flops 2048 | bytes 16384 | tf_op jit(solution)/shard_map/psum | solution.py:20
  528.1 0.0 copy-done.3
  528.1 0.1 fusion.2
  528.3 0.0 copy-start.1
  528.3 15.1 %all-reduce = (f32[2]{0:T(128)S(1)}, f32[2,1280]{1,0:T(2,128)S(1)}) all-reduce(f32[2]{0:T(128)S(1)} %get-tuple-element.7, f32[2,1280]{1,0:T(2,128)S(1)} %get-tuple-element.3), channel_id=1, replica_groups=mesh['row'=4,'col'=8] {'row'}, use_global_device_ids=true, to_apply=%region_6.0 | all-reduce | flops 2562 | bytes 20496 | tf_op jit(solution)/shard_map/psum | solution.py:24
  543.4 0.0 copy-done.2
  543.4 0.0 copy-start
  543.4 5.9 %multiply_reduce_fusion = f32[2]{0:T(128)S(1)} fusion(f32[2,1024,1280]{2,1,0:T(8,128)} %reduce-scatter.2.cloned.1.call-done, f32[2]{0:T(128)S(1)} %broadcast_multiply_fusion, f32[2,1280]{1,0:T(2,128)S(1)} %multiply_add_fusion.1, f32[2,1024]{1,0:T(2,128)S(1)} %get-tuple-element.8), kind=kLoop, calls=%fused_computation.1 | loop fusion | flops 13107198 | bytes 10504208 | tf_op jit(solution)/shard_map/reduce_sum | solution.py:33
  549.4 12.4 %psum.38 = f32[2]{0:T(128)S(1)} all-reduce(f32[2]{0:T(128)S(1)} %multiply_reduce_fusion), channel_id=1, replica_groups=mesh['row'=4,'col'=8] {'row'}, use_global_device_ids=true, to_apply=%region_8.0 | all-reduce | flops 2 | bytes 16 | tf_op jit(solution)/shard_map/psum | solution.py:30
  561.7 12.1 %psum.39 = f32[2]{0:T(128)S(1)} all-reduce(f32[2]{0:T(128)S(1)} %psum.38), channel_id=1, replica_groups=mesh['row'=4,'col'=8] {'col'}, use_global_device_ids=true, to_apply=%region_9.0 | all-reduce | flops 2 | bytes 16 | tf_op jit(solution)/shard_map/psum | solution.py:30
  573.9 9.6 %broadcast_divide_fusion = f32[2,1024,1280]{2,1,0:T(8,128)} fusion(f32[2]{0:T(128)S(1)} %sqrt_maximum_fusion, f32[2,1024,1280]{2,1,0:T(8,128)} %reduce-scatter.2.cloned.1.call-done, f32[2]{0:T(128)S(1)} %broadcast_multiply_fusion, f32[2,1280]{1,0:T(2,128)S(1)} %multiply_add_fusion.1, f32[2,1024]{1,0:T(2,128)S(1)} %get-tuple-element.8), kind=kLoop, calls=%fused_computation.6 | loop fusion | flops 10485760 | bytes 20989968 | tf_op jit(solution)/shard_map/div | solution.py:35
  583.5 0.0 copy-done.1
  583.5 0.0 copy-done
  (3 shorter events, 0.0 us)
Async XLA Ops:
  7.2 504.9 %reduce-scatter.2.cloned.1.call-start = ((), (), s32[]{:S(2)}) async-start(), calls=%async_computation.1 | async-start | bytes 94371840 | tf_op jit(solution)/shard_map/reduce_scatter | solution.py:14
  48.1 480.0 %copy-start.3 = (f32[2,1024]{1,0:T(2,128)S(1)}, f32[2,1024]{1,0:T(2,128)}, u32[]{:S(2)}) copy-start(f32[2,1024]{1,0:T(2,128)} %param.4) | copy-start | bytes 24580
  48.1 495.3 %copy-start.2 = (f32[2,1280]{1,0:T(2,128)S(1)}, f32[2,1280]{1,0:T(2,128)}, u32[]{:S(2)}) copy-start(f32[2,1280]{1,0:T(2,128)} %param.5) | copy-start | bytes 30724
  528.3 55.2 %copy-start.1 = (f32[2,1024]{1,0:T(2,128)}, f32[2,1024]{1,0:T(2,128)S(1)}, u32[]{:S(2)}) copy-start(f32[2,1024]{1,0:T(2,128)S(1)} %get-tuple-element.8) | copy-start | bytes 24580
  543.4 40.0 %copy-start = (f32[2,1280]{1,0:T(2,128)}, f32[2,1280]{1,0:T(2,128)S(1)}, u32[]{:S(2)}) copy-start(f32[2,1280]{1,0:T(2,128)S(1)} %multiply_add_fusion.1) | copy-start | bytes 30724
Sparse Core Ops, SparseCore 0:
  48.2 463.8 reduce-scatter.1
